TPU v7x, 32 devices: a whole 2x2x4 slice. The times are simulated.
32 devices in a mesh: expert: 8 (over z, x), mp: 4 (over y, core).
Axes of the slice: x: 2, y: 2, z: 4, core: 2. Of those that a mesh axis runs over, the one named last changes fastest.
Arguments:
- base_weights: bfloat16 [8, 7168, 1024], P('expert', 'mp'), may hold values from -6 to 6
- deltas: bfloat16 [3, 8, 7168, 1024], P(None, 'expert', 'mp'), may hold values from -1.6 to 1.6
- keep_flags: int32 [3, 8, 896, 8], P(None, 'expert', 'mp'), may hold values 0 or 1
- serve_order: int32 [8], replicated, may hold values from 0 to 7, each once
Outputs:
- served_weights: bfloat16 [8, 1024, 7168], P(None, 'expert', 'mp')
- checksums: float32 [8], P('expert')
- largest_change: float32 [8], P('expert')
Inputs may be any that keep to these rules, and one draw needn't show every extreme that they name: `serve_order`: each expert appears in exactly one slot.
All inputs are finite; a program needn't handle non-finite values. No bound on the sum of `keep_flags` on one device may be relied on, other than what follows from the above.
Results may differ from a plain program's by a relative error of at most 0.008.
Values may be sent and summed in bfloat16 or wider, within the bound.
A program may use at most 64 MiB of HBM per device.

v0:
```python
import functools
import math

import jax
import jax.numpy as jnp
from jax import lax
from jax.experimental import pallas as pl
from jax.experimental.pallas import tpu as pltpu
from jax.sharding import PartitionSpec as P

MESH = pl.DeviceIdType.MESH
LANES = 128


def partner(me, mask, count):
    if count & (count - 1):
        return lax.rem(mask + count - me, count)
    out = 0
    bit = 1
    while bit < count:
        out = out + bit * lax.rem(me // bit + mask // bit, 2)
        bit *= 2
    return out


def exchange_kernel(
    n, m, scale, sub_rows, base_ref, delta_ref, keep_ref, out_ref, stat_ref,
    base_buf, delta_buf, keep_buf, flag_buf, send_buf, acc, stat_buf,
    base_sem, delta_sem, keep_sem, send_sem, recv_sem, stat_send_sem, stat_recv_sem,
):
    e = lax.axis_index("expert")
    p = lax.axis_index("mp")
    rows, columns = base_buf.shape[1], base_ref.shape[2]
    blocks = columns // LANES
    served = columns // n
    per_block = LANES // served
    subs = rows // sub_rows

    barrier = pltpu.get_barrier_semaphore()
    for k in range(1, n):
        pl.semaphore_signal(barrier, inc=1, device_id=(lax.rem(e + k, n), p), device_id_type=MESH)
    for k in range(1, m):
        pl.semaphore_signal(barrier, inc=1, device_id=(e, lax.rem(p + k, m)), device_id_type=MESH)

    def block_at(i):
        mask = blocks - 1 - i // 2 - lax.rem(i, 2) * (blocks // 2)
        return partner(e // per_block, mask, blocks)

    def loads(i, start=0, count=rows, sem=None):
        at = pl.ds(pl.multiple_of(block_at(i) * LANES, LANES), LANES)
        part = pl.ds(start, count)
        sem = i if sem is None else sem
        return (
            pltpu.make_async_copy(base_ref.at[0, part, at], base_buf.at[i, part], base_sem.at[sem]),
            pltpu.make_async_copy(delta_ref.at[:, 0, part, at], delta_buf.at[i, :, part], delta_sem.at[sem]),
        )

    head = loads(0, 0, sub_rows)
    rest = loads(0, sub_rows, rows - sub_rows, blocks)
    keep_load = pltpu.make_async_copy(keep_ref.at[:, 0], keep_buf, keep_sem)

    keep_load.start()
    for copy in head + rest:
        copy.start()
    acc[...] = jnp.zeros_like(acc)
    keep_load.wait()

    def send(i, j, target, lanes, source):
        return pltpu.make_async_remote_copy(
            src_ref=send_buf.at[i, pl.ds(j * served, served), lanes],
            dst_ref=out_ref.at[source, :, lanes],
            send_sem=send_sem.at[target],
            recv_sem=recv_sem.at[source],
            device_id=(target, p),
            device_id_type=MESH,
        )

    def merge(i, row):
        row = pl.multiple_of(row, LANES)
        trimmed = []
        for k in range(3):
            flags = flag_buf[k, pl.ds(pl.multiple_of(row // 8, LANES // 8), LANES // 8), :]
            flags = jnp.broadcast_to(flags[:, None, :], (LANES // 8, 8, LANES)).reshape(LANES, LANES)
            trimmed.append(delta_buf[i, k, pl.ds(row, LANES), :].astype(jnp.float32) * flags)
        total = (trimmed[0] + trimmed[1]) + trimmed[2]
        elected = jnp.where(total > 0, 1.0, jnp.where(total < 0, -1.0, 0.0))
        voters = jnp.zeros((LANES, LANES), jnp.float32)
        size = jnp.zeros((LANES, LANES), jnp.float32)
        for one in trimmed:
            toward = one * elected
            size = size + jnp.maximum(toward, 0.0)
            voters = voters + jnp.where(toward > 0, 1.0, 0.0)
        size = size * jnp.where(voters > 2.5, 1.0 / 3.0, jnp.where(voters > 1.5, 0.5, 1.0))
        base = base_buf[i, pl.ds(row, LANES), :].astype(jnp.float32)
        merged = (base + size * elected).astype(jnp.bfloat16).astype(jnp.float32)
        acc[0] += jnp.sum(merged.reshape(LANES // 8, 8, LANES), axis=0)
        acc[1] = jnp.maximum(acc[1], jnp.max(size.reshape(LANES // 8, 8, LANES), axis=0))
        send_buf[i, :, pl.ds(row, LANES)] = merged.T.astype(jnp.bfloat16)

    def block_step(i, carry):
        block = block_at(i)
        for k in range(3):
            here = keep_buf[k].astype(jnp.float32)
            pick = lax.broadcasted_iota(jnp.int32, (blocks, LANES), 0) == block
            flag_buf[k] = lax.dot_general(
                here, pick.astype(jnp.float32), (((0,), (0,)), ((), ())), preferred_element_type=jnp.float32
            )

        def sub_step(s, carry):
            @pl.when(i + s == 0)
            def _():
                for copy in head:
                    copy.wait()

            @pl.when(i * subs + s == 1)
            def _():
                for copy in rest:
                    copy.wait()

            @pl.when(i * subs - s * blocks * subs > 0)
            def _():
                for copy in loads(i):
                    copy.wait()

            @pl.when(i + 1 + s * blocks < blocks)
            def _():
                for copy in loads(i + 1):
                    copy.start()

            for r in range(sub_rows // LANES):
                merge(i, s * sub_rows + r * LANES)

            @pl.when(i + s == 0)
            def _():
                pl.semaphore_wait(barrier, n + m - 2)

            lanes = pl.ds(pl.multiple_of(s * sub_rows, LANES), sub_rows)
            for j in range(per_block):
                target = block * per_block + j

                @pl.when(target != e)
                def _():
                    send(i, j, target, lanes, e).start()

            return carry

        lax.fori_loop(0, subs, sub_step, 0)
        return carry

    lax.fori_loop(0, blocks, block_step, 0)

    stat_buf[p] = acc[...]

    def stat_copy(k):
        other = lax.rem(p + k, m)
        return other, pltpu.make_async_remote_copy(
            src_ref=acc,
            dst_ref=stat_buf.at[p],
            send_sem=stat_send_sem.at[other],
            recv_sem=stat_recv_sem.at[p],
            device_id=(e, other),
            device_id_type=MESH,
        )

    for k in range(1, m):
        stat_copy(k)[1].start()

    own = e - (e // per_block) * per_block
    for j in range(per_block):

        @pl.when(own == j)
        def _():
            out_ref[e] = send_buf[blocks - 1, pl.ds(j * served, served), :]

    for k in range(1, m):
        other, copy = stat_copy(k)
        copy.wait_send()
        pltpu.make_async_remote_copy(
            src_ref=acc,
            dst_ref=stat_buf.at[other],
            send_sem=stat_send_sem.at[other],
            recv_sem=stat_recv_sem.at[other],
            device_id=(e, other),
            device_id_type=MESH,
        ).wait_recv()
    value = stat_buf[0, 0]
    largest = stat_buf[0, 1]
    for k in range(1, m):
        value = value + stat_buf[k, 0]
        largest = jnp.maximum(largest, stat_buf[k, 1])
    stat_ref[0] = jnp.broadcast_to(jnp.sum(value, keepdims=True) / scale, (8, LANES))
    stat_ref[1] = jnp.broadcast_to(jnp.max(largest, keepdims=True), (8, LANES))

    everything = pl.ds(0, rows)

    def finish(k, carry):
        other = lax.rem(e + k, n)
        copy = send(0, 0, other, everything, other)
        copy.wait_send()
        copy.wait_recv()
        return carry

    lax.fori_loop(1, n, finish, 0)


def serve_kernel(order_ref, held_ref, stat_ref, out_ref, check_ref, largest_ref, check_buf, largest_buf, sems):
    slots = out_ref.shape[0]
    order = order_ref[...].astype(jnp.float32)
    copies = [
        pltpu.make_async_copy(
            held_ref.at[jnp.max(order[0:1, s : s + 1]).astype(jnp.int32)], out_ref.at[s], sems.at[s]
        )
        for s in range(slots)
    ]
    for copy in copies:
        copy.start()
    check_buf[0] = jnp.max(stat_ref[0, 0:1, 0:1])
    largest_buf[0] = jnp.max(stat_ref[1, 0:1, 0:1])
    small = [
        pltpu.make_async_copy(check_buf, check_ref, sems.at[slots]),
        pltpu.make_async_copy(largest_buf, largest_ref, sems.at[slots + 1]),
    ]
    for copy in small:
        copy.start()
    for copy in copies + small:
        copy.wait()


def in_hbm(x):
    return pltpu.with_memory_space_constraint(x, pltpu.HBM)


def on_device(n, m, base_weights, deltas, keep_flags, serve_order):
    _, rows, columns = base_weights.shape
    blocks = columns // LANES
    served = columns // n
    sub_rows = 2 * LANES if rows % (2 * LANES) == 0 else LANES
    hbm = pl.BlockSpec(memory_space=pltpu.HBM)
    vmem = pl.BlockSpec(memory_space=pltpu.VMEM)
    held, stats = pl.pallas_call(
        functools.partial(exchange_kernel, n, m, math.sqrt(rows * m * columns), sub_rows),
        out_shape=(
            jax.ShapeDtypeStruct((n, served, rows), jnp.bfloat16),
            jax.ShapeDtypeStruct((2, 8, LANES), jnp.float32),
        ),
        in_specs=[hbm] * 3,
        out_specs=(vmem, vmem),
        scratch_shapes=[
            pltpu.VMEM((blocks, rows, LANES), jnp.bfloat16),
            pltpu.VMEM((blocks, 3, rows, LANES), jnp.bfloat16),
            pltpu.VMEM((3, blocks, rows // 8), jnp.int32),
            pltpu.VMEM((3, rows // 8, LANES), jnp.float32),
            pltpu.VMEM((blocks, LANES, rows), jnp.bfloat16),
            pltpu.VMEM((2, 8, LANES), jnp.float32),
            pltpu.VMEM((m, 2, 8, LANES), jnp.float32),
            pltpu.SemaphoreType.DMA((blocks + 1,)),
            pltpu.SemaphoreType.DMA((blocks + 1,)),
            pltpu.SemaphoreType.DMA,
            pltpu.SemaphoreType.DMA((n,)),
            pltpu.SemaphoreType.DMA((n,)),
            pltpu.SemaphoreType.DMA((m,)),
            pltpu.SemaphoreType.DMA((m,)),
        ],
        compiler_params=pltpu.CompilerParams(
            collective_id=0, has_side_effects=True, vmem_limit_bytes=49 * 1024 * 1024
        ),
        name="exchange",
    )(in_hbm(base_weights), in_hbm(deltas), in_hbm(jnp.swapaxes(keep_flags, 2, 3)))
    return pl.pallas_call(
        serve_kernel,
        out_shape=(
            jax.ShapeDtypeStruct((n, served, rows), jnp.bfloat16),
            jax.ShapeDtypeStruct((1,), jnp.float32),
            jax.ShapeDtypeStruct((1,), jnp.float32),
        ),
        in_specs=[vmem, vmem, vmem],
        out_specs=(hbm, hbm, hbm),
        scratch_shapes=[
            pltpu.SMEM((1,), jnp.float32),
            pltpu.SMEM((1,), jnp.float32),
            pltpu.SemaphoreType.DMA((n + 2,)),
        ],
        compiler_params=pltpu.CompilerParams(vmem_limit_bytes=8 * 1024 * 1024),
        name="serve",
    )(serve_order.reshape(1, n), held, stats)


def solution(mesh):
    n, m = mesh.shape["expert"], mesh.shape["mp"]
    in_specs = (
        P("expert", "mp", None),
        P(None, "expert", "mp", None),
        P(None, "expert", "mp", None),
        P(),
    )
    out_specs = (P(None, "expert", "mp"), P("expert"), P("expert"))
    return jax.shard_map(
        functools.partial(on_device, n, m), mesh=mesh, in_specs=in_specs, out_specs=out_specs, check_vma=False
    )
```

profile of v0, /device:TPU:0, one launch (start us, length us, event | category | flops | bytes accessed | tf_op | source)
XLA Modules:
  0.0 95.4 jit_solution(5915576446351783118)
XLA Ops:
  0.6 0.0 copy-start
  0.6 92.8 %exchange.1 = (bf16[8,128,1792]{2,1,0:T(8,128)(2,1)S(1)}, f32[2,8,128]{2,1,0:T(8,128)S(1)}) custom-call(bf16[1,1792,1024]{2,1,0:T(8,128)(2,1)} %base_ref.1, bf16[3,1,1792,1024]{3,2,1,0:T(8,128)(2,1)} %delta_ref.1, s32[3,1,8,224]{3,2,1,0:T(8,128)} %bitcast.3), custom_call_target="tpu_custom_call" | custom-call | tf_op jit(solution)/shard_map/exchange/pallas_call | solution.py:240
  93.4 0.0 copy-done
  93.4 2.0 %serve.1 = (bf16[8,128,1792]{2,1,0:T(8,128)(2,1)}, f32[1]{0:T(128)}, f32[1]{0:T(128)}) custom-call(s32[1,8]{1,0:T(1,128)S(1)} %bitcast.2, bf16[8,128,1792]{2,1,0:T(8,128)(2,1)S(1)} %get-tuple-element.5.held_ref, f32[2,8,128]{2,1,0:T(8,128)S(1)} %get-tuple-element.6.stat_ref), custom_call_target="tpu_custom_call" | custom-call | tf_op jit(solution)/shard_map/serve/pallas_call | solution.py:269
Async XLA Ops:
  0.6 92.8 %copy-start = (s32[8]{0:T(128)S(1)}, s32[8]{0:T(128)}, u32[]{:S(2)}) copy-start(s32[8]{0:T(128)} %param.7) | copy-start | bytes 100
where the time goes:
time: 95.5 us; the launch traced here: 95.4 us
  Pallas kernels  94.7 us (99%)
    pallas_call x1, Pallas kernels, on_device(): pl.pallas_call(functools.partial(exchange_kernel, n, m, math.sqrt(rows *...  92.8 us
    pallas_call x1, Pallas kernels, on_device(): pl.pallas_call(serve_kernel, out_shape=(jax.ShapeDtypeStruct((n, served,...  1.97 us

commit v1 on v0

--- a/solution.py
+++ b/solution.py
@@ -43,7 +43,11 @@
         pl.semaphore_signal(barrier, inc=1, device_id=(e, lax.rem(p + k, m)), device_id_type=MESH)
 
     def block_at(i):
-        mask = blocks - 1 - i // 2 - lax.rem(i, 2) * (blocks // 2)
+        if blocks % 2:
+            return partner(e // per_block, lax.rem(i + 1, blocks), blocks)
+        half = blocks // 2
+        late = i // half
+        mask = (1 - late) * (half + i) + late * lax.rem(i + 1, half)
         return partner(e // per_block, mask, blocks)
 
     def loads(i, start=0, count=rows, sem=None):

time: 95.5 us -> 87 us (0.911)
  the two profiles are of different devices: /device:TPU:0 before, /device:TPU:10 now
where the time goes in v1:
time: 87 us; the launch traced here: 86.3 us
  Pallas kernels  85.6 us (98%)
    pallas_call x1, Pallas kernels, on_device(): pl.pallas_call(functools.partial(exchange_kernel, n, m, math.sqrt(rows *...  83.6 us
    pallas_call x1, Pallas kernels, on_device(): pl.pallas_call(serve_kernel, out_shape=(jax.ShapeDtypeStruct((n, served,...  1.97 us

profile of v1, /device:TPU:10, one launch (start us, length us, event | category | flops | bytes accessed | tf_op | source)
XLA Modules:
  0.0 86.3 jit_solution(488867084635442317)
XLA Ops:
  0.6 0.0 copy-start
  0.6 83.6 %exchange.1 = (bf16[8,128,1792]{2,1,0:T(8,128)(2,1)S(1)}, f32[2,8,128]{2,1,0:T(8,128)S(1)}) custom-call(bf16[1,1792,1024]{2,1,0:T(8,128)(2,1)} %base_ref.1, bf16[3,1,1792,1024]{3,2,1,0:T(8,128)(2,1)} %delta_ref.1, s32[3,1,8,224]{3,2,1,0:T(8,128)} %bitcast.3), custom_call_target="tpu_custom_call" | custom-call | tf_op jit(solution)/shard_map/exchange/pallas_call | solution.py:244
  84.3 0.0 copy-done
  84.3 2.0 %serve.1 = (bf16[8,128,1792]{2,1,0:T(8,128)(2,1)}, f32[1]{0:T(128)}, f32[1]{0:T(128)}) custom-call(s32[1,8]{1,0:T(1,128)S(1)} %bitcast.2, bf16[8,128,1792]{2,1,0:T(8,128)(2,1)S(1)} %get-tuple-element.5.held_ref, f32[2,8,128]{2,1,0:T(8,128)S(1)} %get-tuple-element.6.stat_ref), custom_call_target="tpu_custom_call" | custom-call | tf_op jit(solution)/shard_map/serve/pallas_call | solution.py:273
Async XLA Ops:
  0.6 83.6 %copy-start = (s32[8]{0:T(128)S(1)}, s32[8]{0:T(128)}, u32[]{:S(2)}) copy-start(s32[8]{0:T(128)} %param.7) | copy-start | bytes 100

commit v2 on v0

--- a/solution.py
+++ b/solution.py
@@ -27,6 +27,7 @@
     n, m, scale, sub_rows, base_ref, delta_ref, keep_ref, out_ref, stat_ref,
     base_buf, delta_buf, keep_buf, flag_buf, send_buf, acc, stat_buf,
     base_sem, delta_sem, keep_sem, send_sem, recv_sem, stat_send_sem, stat_recv_sem,
+    known_sem,
 ):
     e = lax.axis_index("expert")
     p = lax.axis_index("mp")
@@ -36,15 +37,20 @@
     per_block = LANES // served
     subs = rows // sub_rows
 
-    barrier = pltpu.get_barrier_semaphore()
-    for k in range(1, n):
-        pl.semaphore_signal(barrier, inc=1, device_id=(lax.rem(e + k, n), p), device_id_type=MESH)
-    for k in range(1, m):
-        pl.semaphore_signal(barrier, inc=1, device_id=(e, lax.rem(p + k, m)), device_id_type=MESH)
+    half, quarter = blocks // 2, blocks // 4
+    mine = e // per_block
+    lower = 1 - mine // half
+    inner = lax.rem(mine // quarter + mine // half, 2)
+    facing_inner = lower * half + (1 - lower) * quarter
+    facing_outer = lower * (half + quarter)
+    beside = partner(e, quarter * per_block, n)
 
     def block_at(i):
-        mask = blocks - 1 - i // 2 - lax.rem(i, 2) * (blocks // 2)
-        return partner(e // per_block, mask, blocks)
+        stage = (i + quarter - 1) // quarter
+        at_outer = stage * (2 - stage)
+        far = at_outer * (facing_outer + i - 1) + (1 - at_outer) * facing_inner + stage // 2 * (i - quarter)
+        near = partner(mine, lax.rem(i + 1, half), blocks)
+        return (1 - i // half) * far + i // half * near
 
     def loads(i, start=0, count=rows, sem=None):
         at = pl.ds(pl.multiple_of(block_at(i) * LANES, LANES), LANES)
@@ -62,6 +68,27 @@
     keep_load.start()
     for copy in head + rest:
         copy.start()
+
+    barrier = pltpu.get_barrier_semaphore()
+
+    def greet(expert, place):
+        pl.semaphore_signal(barrier, inc=1, device_id=(expert, place), device_id_type=MESH)
+
+    @pl.when(inner - lax.rem(mine, quarter) == 1)
+    def _():
+        for k in range(quarter * per_block):
+            greet(facing_inner * per_block + k, p)
+
+    for k in range(1, n):
+        other = lax.rem(e + k, n)
+        block = other // per_block
+
+        @pl.when(lax.rem(block // quarter + block // half, 2) == 0)
+        def _():
+            greet(other, p)
+
+    for k in range(1, m):
+        greet(inner * beside + (1 - inner) * e, lax.rem(p + k, m))
     acc[...] = jnp.zeros_like(acc)
     keep_load.wait()
 
@@ -130,9 +157,18 @@
             for r in range(sub_rows // LANES):
                 merge(i, s * sub_rows + r * LANES)
 
-            @pl.when(i + s == 0)
-            def _():
-                pl.semaphore_wait(barrier, n + m - 2)
+            @pl.when(i + s + inner == 0)
+            def _():
+                pl.semaphore_wait(barrier, n - 1 + 2 * (m - 1))
+                pl.semaphore_signal(known_sem, inc=1, device_id=(beside, p), device_id_type=MESH)
+
+            @pl.when(i + s - inner == -1)
+            def _():
+                pl.semaphore_wait(barrier, per_block)
+
+            @pl.when((i * subs + s) * inner == subs)
+            def _():
+                pl.semaphore_wait(known_sem, 1)
 
             lanes = pl.ds(pl.multiple_of(s * sub_rows, LANES), sub_rows)
             for j in range(per_block):
@@ -260,6 +296,7 @@
             pltpu.SemaphoreType.DMA((n,)),
             pltpu.SemaphoreType.DMA((m,)),
             pltpu.SemaphoreType.DMA((m,)),
+            pltpu.SemaphoreType.REGULAR,
         ],
         compiler_params=pltpu.CompilerParams(
             collective_id=0, has_side_effects=True, vmem_limit_bytes=49 * 1024 * 1024

time: 95.5 us -> 85.5 us (0.90)
  the two profiles are of different devices: /device:TPU:0 before, /device:TPU:10 now
where the time goes in v2:
time: 85.5 us; the launch traced here: 85.4 us
  Pallas kernels  84.7 us (99%)
    pallas_call x1, Pallas kernels, on_device(): pl.pallas_call(functools.partial(exchange_kernel, n, m, math.sqrt(rows *...  82.7 us
    pallas_call x1, Pallas kernels, on_device(): pl.pallas_call(serve_kernel, out_shape=(jax.ShapeDtypeStruct((n, served,...  1.97 us

profile of v2, /device:TPU:10, one launch (start us, length us, event | category | flops | bytes accessed | tf_op | source)
XLA Modules:
  0.0 85.4 jit_solution(12990354918433748445)
XLA Ops:
  0.6 0.0 copy-start
  0.6 82.7 %exchange.1 = (bf16[8,128,1792]{2,1,0:T(8,128)(2,1)S(1)}, f32[2,8,128]{2,1,0:T(8,128)S(1)}) custom-call(bf16[1,1792,1024]{2,1,0:T(8,128)(2,1)} %base_ref.1, bf16[3,1,1792,1024]{3,2,1,0:T(8,128)(2,1)} %delta_ref.1, s32[3,1,8,224]{3,2,1,0:T(8,128)} %bitcast.3), custom_call_target="tpu_custom_call" | custom-call | tf_op jit(solution)/shard_map/exchange/pallas_call | solution.py:276
  83.4 0.0 copy-done
  83.4 2.0 %serve.1 = (bf16[8,128,1792]{2,1,0:T(8,128)(2,1)}, f32[1]{0:T(128)}, f32[1]{0:T(128)}) custom-call(s32[1,8]{1,0:T(1,128)S(1)} %bitcast.2, bf16[8,128,1792]{2,1,0:T(8,128)(2,1)S(1)} %get-tuple-element.5.held_ref, f32[2,8,128]{2,1,0:T(8,128)S(1)} %get-tuple-element.6.stat_ref), custom_call_target="tpu_custom_call" | custom-call | tf_op jit(solution)/shard_map/serve/pallas_call | solution.py:306
Async XLA Ops:
  0.6 82.8 %copy-start = (s32[8]{0:T(128)S(1)}, s32[8]{0:T(128)}, u32[]{:S(2)}) copy-start(s32[8]{0:T(128)} %param.7) | copy-start | bytes 100

commit v3 on v2

--- a/solution.py
+++ b/solution.py
@@ -229,14 +229,24 @@
 
     everything = pl.ds(0, rows)
 
-    def finish(k, carry):
-        other = lax.rem(e + k, n)
-        copy = send(0, 0, other, everything, other)
-        copy.wait_send()
-        copy.wait_recv()
-        return carry
-
-    lax.fori_loop(1, n, finish, 0)
+    order = [*range(half, blocks), *range(1, quarter + 1), *range(quarter + 1, half), 0]
+    for i in order:
+        block = block_at(i)
+        for j in range(per_block):
+            other = block * per_block + j
+
+            @pl.when(other != e)
+            def _():
+                send(0, 0, other, everything, other).wait_send()
+
+    for i in order:
+        block = block_at(i)
+        for j in range(per_block):
+            other = block * per_block + j
+
+            @pl.when(other != e)
+            def _():
+                send(0, 0, other, everything, other).wait_recv()
 
 
 def serve_kernel(order_ref, held_ref, stat_ref, out_ref, check_ref, largest_ref, check_buf, largest_buf, sems):

time: 85.5 us -> 85.5 us (level)
  no operation moved by 1% of the time
where the time goes in v3:
time: 85.5 us; the launch traced here: 85.4 us
  Pallas kernels  84.7 us (99%)
    pallas_call x1, Pallas kernels, on_device(): pl.pallas_call(functools.partial(exchange_kernel, n, m, math.sqrt(rows *...  82.7 us
    pallas_call x1, Pallas kernels, on_device(): pl.pallas_call(serve_kernel, out_shape=(jax.ShapeDtypeStruct((n, served,...  1.97 us

profile of v3, /device:TPU:10, one launch (start us, length us, event | category | flops | bytes accessed | tf_op | source)
XLA Modules:
  0.0 85.4 jit_solution(13251770375523869803)
XLA Ops:
  0.6 0.0 copy-start
  0.6 82.7 %exchange.1 = (bf16[8,128,1792]{2,1,0:T(8,128)(2,1)S(1)}, f32[2,8,128]{2,1,0:T(8,128)S(1)}) custom-call(bf16[1,1792,1024]{2,1,0:T(8,128)(2,1)} %base_ref.1, bf16[3,1,1792,1024]{3,2,1,0:T(8,128)(2,1)} %delta_ref.1, s32[3,1,8,224]{3,2,1,0:T(8,128)} %bitcast.3), custom_call_target="tpu_custom_call" | custom-call | tf_op jit(solution)/shard_map/exchange/pallas_call | solution.py:286
  83.4 0.0 copy-done
  83.4 2.0 %serve.1 = (bf16[8,128,1792]{2,1,0:T(8,128)(2,1)}, f32[1]{0:T(128)}, f32[1]{0:T(128)}) custom-call(s32[1,8]{1,0:T(1,128)S(1)} %bitcast.2, bf16[8,128,1792]{2,1,0:T(8,128)(2,1)S(1)} %get-tuple-element.5.held_ref, f32[2,8,128]{2,1,0:T(8,128)S(1)} %get-tuple-element.6.stat_ref), custom_call_target="tpu_custom_call" | custom-call | tf_op jit(solution)/shard_map/serve/pallas_call | solution.py:316
Async XLA Ops:
  0.6 82.7 %copy-start = (s32[8]{0:T(128)S(1)}, s32[8]{0:T(128)}, u32[]{:S(2)}) copy-start(s32[8]{0:T(128)} %param.7) | copy-start | bytes 100

commit v4 on v3

--- a/solution.py
+++ b/solution.py
@@ -170,13 +170,22 @@
             def _():
                 pl.semaphore_wait(known_sem, 1)
 
-            lanes = pl.ds(pl.multiple_of(s * sub_rows, LANES), sub_rows)
-            for j in range(per_block):
-                target = block * per_block + j
-
-                @pl.when(target != e)
-                def _():
-                    send(i, j, target, lanes, e).start()
+            def send_rows(start, count):
+                lanes = pl.ds(pl.multiple_of(start, LANES), count)
+                for j in range(per_block):
+                    target = block * per_block + j
+
+                    @pl.when(target != e)
+                    def _():
+                        send(i, j, target, lanes, e).start()
+
+            @pl.when(i == 0)
+            def _():
+                send_rows(s * sub_rows, sub_rows)
+
+            @pl.when((i > 0) & (s == subs - 1))
+            def _():
+                send_rows(0, rows)
 
             return carry
 

time: 85.5 us -> 85.5 us (level)
  no operation moved by 1% of the time
where the time goes in v4:
time: 85.5 us; the launch traced here: 85.4 us
  Pallas kernels  84.7 us (99%)
    pallas_call x1, Pallas kernels, on_device(): pl.pallas_call(functools.partial(exchange_kernel, n, m, math.sqrt(rows *...  82.7 us
    pallas_call x1, Pallas kernels, on_device(): pl.pallas_call(serve_kernel, out_shape=(jax.ShapeDtypeStruct((n, served,...  1.97 us

profile of v4, /device:TPU:10, one launch (start us, length us, event | category | flops | bytes accessed | tf_op | source)
XLA Modules:
  0.0 85.4 jit_solution(7446672852694197389)
XLA Ops:
  0.6 0.0 copy-start
  0.6 82.7 %exchange.1 = (bf16[8,128,1792]{2,1,0:T(8,128)(2,1)S(1)}, f32[2,8,128]{2,1,0:T(8,128)S(1)}) custom-call(bf16[1,1792,1024]{2,1,0:T(8,128)(2,1)} %base_ref.1, bf16[3,1,1792,1024]{3,2,1,0:T(8,128)(2,1)} %delta_ref.1, s32[3,1,8,224]{3,2,1,0:T(8,128)} %bitcast.3), custom_call_target="tpu_custom_call" | custom-call | tf_op jit(solution)/shard_map/exchange/pallas_call | solution.py:295
  83.4 0.0 copy-done
  83.4 2.0 %serve.1 = (bf16[8,128,1792]{2,1,0:T(8,128)(2,1)}, f32[1]{0:T(128)}, f32[1]{0:T(128)}) custom-call(s32[1,8]{1,0:T(1,128)S(1)} %bitcast.2, bf16[8,128,1792]{2,1,0:T(8,128)(2,1)S(1)} %get-tuple-element.5.held_ref, f32[2,8,128]{2,1,0:T(8,128)S(1)} %get-tuple-element.6.stat_ref), custom_call_target="tpu_custom_call" | custom-call | tf_op jit(solution)/shard_map/serve/pallas_call | solution.py:325
Async XLA Ops:
  0.6 82.8 %copy-start = (s32[8]{0:T(128)S(1)}, s32[8]{0:T(128)}, u32[]{:S(2)}) copy-start(s32[8]{0:T(128)} %param.7) | copy-start | bytes 100
